TPU v7x, 32 devices: a whole 2x2x4 slice. The times are simulated.
32 devices in a mesh: rep: 2 (over y), exp: 4 (over x, core), tp: 4 (over z).
Axes of the slice: x: 2, y: 2, z: 4, core: 2. Of those that a mesh axis runs over, the one named last changes fastest.
Arguments:
- tokens: bfloat16 [256, 6144], P(('rep', 'exp'), 'tp'), parts along dimension 0, may hold values from -6 to 6
- expert_ids: int32 [256, 2], P(('rep', 'exp')), parts along dimension 0, may hold values from 0 to 3, all different within a row; in each aligned block of 32 rows (0 to 31, 32 to 63, ...) at most 20 rows name the same one
- route_logits: float32 [256, 2], P(('rep', 'exp')), parts along dimension 0, may hold values from -6 to 6
- gate_weight: bfloat16 [6144, 32768], P(None, ('exp', 'tp')), may hold values from -0.078125 to 0.078125
- up_weight: bfloat16 [6144, 32768], P(None, ('exp', 'tp')), may hold values from -0.078125 to 0.078125
- down_weight: bfloat16 [32768, 6144], P(('exp', 'tp')), may hold values from -0.0625 to 0.0625
Outputs:
- moe_out: bfloat16 [256, 6144], P(('rep', 'exp'), 'tp'), parts along dimension 0
There are 2 independent parts, one for each index of `rep`. A program takes and returns all parts, laid end to end along the dimension named above; an argument that names none is the same for every part. Nothing has to cross between parts.
Inputs may be any that keep to these rules, and one draw needn't show every extreme that they name: `expert_ids`: each token names two different experts. In each aligned block of 32 tokens no expert is named by more than 20 tokens, a bound that some block reaches.
All inputs are finite; a program needn't handle non-finite values.
Results may differ from a plain program's by a relative error of at most 0.019.
Values may be sent and summed in bfloat16 or wider, within the bound.
A program may use at most 128 MiB of HBM per device.

v0:
```python
import jax
import jax.numpy as jnp
from jax import lax
from jax.sharding import PartitionSpec as P

D = 6144
EXPERTS = 4
CAP = 20


def slot_tables(expert_ids, route_logits):
    chosen = (expert_ids[:, :, None] == jnp.arange(EXPERTS, dtype=jnp.int32)[None, None, :]).astype(
        jnp.int32
    )
    per_token = jnp.sum(chosen, axis=1)
    before = jnp.cumsum(per_token, axis=0) - per_token
    position = jnp.sum(chosen * before[:, None, :], axis=2)
    at_slot = (position[:, :, None] == jnp.arange(CAP, dtype=jnp.int32)[None, None, :]).astype(
        jnp.float32
    )
    chosen_f = chosen.astype(jnp.float32)
    diff = route_logits[:, 0] - route_logits[:, 1]
    shares = jnp.stack([jax.nn.sigmoid(diff), jax.nn.sigmoid(-diff)], axis=1)
    placement = jnp.einsum("tke,tkc->ect", chosen_f, at_slot)
    mixing = jnp.einsum("tk,tke,tkc->tec", shares, chosen_f, at_slot)
    return (placement.astype(jnp.bfloat16), mixing)


def on_device(tokens, expert_ids, route_logits, gate_weight, up_weight, down_weight):
    exp_count = lax.axis_size("exp")
    groups = exp_count // EXPERTS
    placement, mixing = slot_tables(expert_ids, route_logits)
    whole_rows = lax.all_gather(tokens, "tp", axis=1, tiled=True)
    slots = jnp.einsum(
        "ect,td->ecd", placement, whole_rows, preferred_element_type=jnp.float32
    ).astype(jnp.bfloat16)
    outgoing = jnp.repeat(slots, groups, axis=0)
    gathered = lax.all_to_all(outgoing, "exp", split_axis=0, concat_axis=0, tiled=True)
    slot_rows = gathered.reshape(exp_count * CAP, D)
    gate_act = jnp.dot(slot_rows, gate_weight, preferred_element_type=jnp.float32)
    up_act = jnp.dot(slot_rows, up_weight, preferred_element_type=jnp.float32)
    hidden = (jax.nn.silu(gate_act) * up_act).astype(jnp.bfloat16)
    partial_value = jnp.dot(hidden, down_weight, preferred_element_type=jnp.float32).astype(
        jnp.bfloat16
    )
    partial_value = lax.optimization_barrier(partial_value).reshape(exp_count, CAP, D)
    narrow = lax.psum_scatter(
        partial_value.astype(jnp.float32).astype(jnp.bfloat16),
        "tp",
        scatter_dimension=2,
        tiled=True,
    ).astype(jnp.float32)
    returned = lax.all_to_all(
        narrow.astype(jnp.bfloat16), "exp", split_axis=0, concat_axis=0, tiled=True
    ).astype(narrow.dtype)
    summed = jnp.sum(returned.reshape(EXPERTS, groups, CAP, returned.shape[2]), axis=1)
    moe_out = jnp.einsum("tec,ecd->td", mixing, summed, precision=lax.Precision.HIGHEST).astype(
        jnp.bfloat16
    )
    return moe_out


def solution(mesh):
    return jax.shard_map(
        on_device,
        mesh=mesh,
        in_specs=(
            P(("rep", "exp"), "tp"),
            P(("rep", "exp"), None),
            P(("rep", "exp"), None),
            P(None, ("exp", "tp")),
            P(None, ("exp", "tp")),
            P(("exp", "tp"), None),
        ),
        out_specs=P(("rep", "exp"), "tp"),
        check_vma=False,
    )
```

profile of v0, /device:TPU:0, one launch (start us, length us, event | category | flops | bytes accessed | tf_op | source)
XLA Modules:
  0.0 124.6 jit_solution(4549421285769029820)
XLA Ops:
  6.5 0.0 reduce-scatter.2.cloned.1.call-start
  6.5 0.7 convert_reduce_fusion
  7.2 0.7 convert_convert_fusion
  7.9 0.1 copy.11
  8.0 0.1 reduce_window_sum.11
  8.1 0.1 copy.13
  8.1 0.7 select_reduce_fusion
  8.8 0.1 copy.14
  8.9 0.1 copy.16
  9.0 16.5 %all_gather.3 = bf16[32,6144]{1,0:T(8,128)(2,1)S(1)} all-gather(bf16[32,1536]{1,0:T(8,128)(2,1)} %param.6), channel_id=1, replica_groups=mesh['rep'=2,'exp'=4,'tp'=4] {'tp'}, dimensions={1}, use_global_device_ids=true | all-gather | bytes 491520 | tf_op jit(solution)/shard_map/all_gather | solution.py:33
  25.5 0.3 fusion.2
  25.8 0.5 convolution_convert_fusion
  26.3 18.4 %all_to_all.10 = bf16[4,20,6144]{2,1,0:T(8,128)(2,1)S(1)} all-to-all(bf16[4,20,6144]{2,1,0:T(8,128)(2,1)S(1)} %convolution_convert_fusion), channel_id=1, replica_groups=mesh['rep'=2,'exp'=4,'tp'=4] {'exp'}, dimensions={0} | all-to-all | bytes 1966080 | tf_op jit(solution)/shard_map/all_to_all | solution.py:38
  44.7 0.3 reshape.20
  45.0 10.5 %fusion.16 = f32[80,2048]{1,0:T(8,128)S(1)} fusion(bf16[80,6144]{1,0:T(8,128)(2,1)S(1)} %reshape.20, bf16[6144,2048]{1,0:T(8,128)(2,1)} %param.9), kind=kOutput, calls=%fused_computation.31 | convolution fusion | flops 2013265920 | bytes 26804224 | tf_op jit(solution)/shard_map/dot_general | solution.py:40
  55.4 0.0 copy-start.1
  55.4 0.0 copy-start
  55.5 19.9 %convolution_convert_fusion.1 = bf16[80,6144]{1,0:T(8,128)(2,1)S(1)} fusion(bf16[2048,6144]{1,0:T(8,128)(2,1)} %param.11, bf16[80,6144]{1,0:T(8,128)(2,1)S(1)} %reshape.20, bf16[6144,2048]{1,0:T(8,128)(2,1)} %param.10, f32[80,2048]{1,0:T(8,128)S(1)} %fusion.16), kind=kOutput, calls=%fused_computation.1 | convolution fusion | flops 4028006400 | bytes 52953088 | tf_op jit(solution)/shard_map/dot_general | solution.py:43
  75.4 1.1 reshape.21
  76.5 0.0 reduce-scatter.2.cloned.1.call-update
  76.5 0.0 copy-done.1
  76.6 0.0 copy-done
  76.6 0.1 copy.15
  76.7 30.1 %reduce-scatter.2.cloned.1.call-done = bf16[4,20,1536]{2,1,0:T(8,128)(2,1)} async-done(((bf16[4,20,6144]{2,1,0:T(8,128)(2,1)}), bf16[4,20,1536]{2,1,0:T(8,128)(2,1)}) %reduce-scatter.2.cloned.1.call-update) | async-done | bytes 245776 | tf_op jit(solution)/shard_map/reduce_scatter | solution.py:47
  106.9 3.5 %all-to-all-start.1 = ((bf16[4,20,1536]{2,1,0:T(8,128)(2,1)}), bf16[4,20,1536]{2,1,0:T(8,128)(2,1)S(1)}, u32[]{:S(2)}, u32[]{:S(2)}) async-start(bf16[4,20,1536]{2,1,0:T(8,128)(2,1)} %reduce-scatter.2.cloned.1.call-done), calls=%async_computation.2 | async-start | bytes 589824 | tf_op jit(solution)/shard_map/all_to_all | solution.py:53
  110.3 0.3 fusion.12
  110.6 6.1 %all-to-all-done.1 = bf16[4,20,1536]{2,1,0:T(8,128)(2,1)S(1)} async-done(((bf16[4,20,1536]{2,1,0:T(8,128)(2,1)}), bf16[4,20,1536]{2,1,0:T(8,128)(2,1)S(1)}, u32[]{:S(2)}, u32[]{:S(2)}) %all-to-all-start.1) | async-done | bytes 245792 | tf_op jit(solution)/shard_map/all_to_all | solution.py:53
  116.6 1.1 fusion.1
  (4 shorter events, 0.0 us)
Async XLA Ops:
  6.5 100.3 %reduce-scatter.2.cloned.1.call-start = ((), (), s32[]{:S(2)}) async-start(), calls=%async_computation.3 | async-start | bytes 1474560 | tf_op jit(solution)/shard_map/reduce_scatter | solution.py:47
  55.4 21.1 %copy-start.1 = (f32[32,2]{0,1:T(2,128)S(1)}, f32[32,2]{0,1:T(2,128)}, u32[]{:S(2)}) copy-start(f32[32,2]{0,1:T(2,128)} %param.8) | copy-start | bytes 772
  55.4 21.1 %copy-start = (s32[32,2]{0,1:T(2,128)S(1)}, s32[32,2]{0,1:T(2,128)}, u32[]{:S(2)}) copy-start(s32[32,2]{0,1:T(2,128)} %param.7) | copy-start | bytes 772
  106.9 9.8 %all-to-all-start.1 = ((bf16[4,20,1536]{2,1,0:T(8,128)(2,1)}), bf16[4,20,1536]{2,1,0:T(8,128)(2,1)S(1)}, u32[]{:S(2)}, u32[]{:S(2)}) async-start(bf16[4,20,1536]{2,1,0:T(8,128)(2,1)} %reduce-scatter.2.cloned.1.call-done), calls=%async_computation.2 | async-start | bytes 589824 | tf_op jit(solution)/shard_map/all_to_all | solution.py:53
Sparse Core Ops, SparseCore 0:
  76.7 30.1 reduce-scatter.1
where the time goes:
time: 125 us
  waiting for transfers between devices  36.2 us (29%)
  blocking collectives  34.9 us (28%)
  matrix products  32.5 us (26%)
  between operations  13.5 us (11%)
  starting transfers between devices  3.45 us (3%)
  other arithmetic  2.17 us (2%)
  local copies, waits for them, and re-layouts  1.89 us (2%)
    reduce_scatter x1, waiting for transfers between devices, on_device(): lax.psum_scatter(partial_value.astype(jnp.float32).astype(jnp.bfloat16),...  30.1 us
    dot_general x1, matrix products, on_device(): jnp.dot(hidden, down_weight, preferred_element_type=jnp.float32)  19.9 us
    all_to_all x1, blocking collectives, on_device(): lax.all_to_all(outgoing, 'exp', split_axis=0, concat_axis=0, tiled=True)  18.4 us
    all_gather x1, blocking collectives, on_device(): whole_rows = lax.all_gather(tokens, 'tp', axis=1, tiled=True)  16.5 us
    dot_general x1, matrix products, on_device(): jnp.dot(slot_rows, gate_weight, preferred_element_type=jnp.float32)  10.5 us
    all_to_all x1, waiting for transfers between devices, on_device(): lax.all_to_all(narrow.astype(jnp.bfloat16), 'exp', split_axis=0, concat_a...  6.06 us
    all_to_all x1, starting transfers between devices, on_device(): lax.all_to_all(narrow.astype(jnp.bfloat16), 'exp', split_axis=0, concat_a...  3.45 us
  transfers between devices with their start and end apart: 2, of which 2 were waited for; matrix products, arithmetic and copies ran while one was open for 0% of the time, Pallas kernels for 0%

commit v1 on v0

v1 whole, which is shorter than its diff:
```python
import functools

import jax
import jax.numpy as jnp
from jax import lax
from jax.experimental import pallas as pl
from jax.experimental.pallas import tpu as pltpu
from jax.sharding import PartitionSpec as P

EXPERTS = 4
CORES = 2
MESH = pl.DeviceIdType.MESH
F32 = jnp.float32
BF16 = jnp.bfloat16


def near_first(n):
    order = [0]
    for d in range(1, n // 2 + 1):
        for v in (d, n - d):
            if v not in order:
                order.append(v)
    return order


def tile_of(n):
    return next(t for t in (512, 384, 256, 128) if n % t == 0)


def kernel(
    n_exp,
    n_tp,
    n_w,
    tok_ref,
    ids_ref,
    log_ref,
    gate_hbm,
    up_hbm,
    down_hbm,
    out_ref,
    gate_w,
    up_w,
    down_w,
    rows,
    acc_g,
    acc_u,
    hidden,
    share,
    wcol,
    psend,
    precv,
    comb,
    xrecv,
    zsend,
    zrecv,
    gate_sem,
    up_sem,
    down_sem,
    in_z,
    in_x,
    in_p,
    share_x,
    share_p,
    out_p,
    out_x,
    out_z,
):
    n_x = n_exp // CORES
    tok, dc = tok_ref.shape
    width = acc_g.shape[1]
    half = n_x * tok
    me = lax.axis_index("exp")
    z = lax.axis_index("tp")
    x = me // CORES
    core = me % CORES
    partner = x * CORES + (1 - core)
    peers = [lax.rem(x + k, n_x) for k in range(1, n_x)]
    order = near_first(n_tp)
    out_order = order[::-1]
    mine = pl.ds(pl.multiple_of(x * tok, tok), tok)

    def remote(src, dst, sems, idx, device):
        return pltpu.make_async_remote_copy(
            src_ref=src,
            dst_ref=dst,
            send_sem=sems.at[(0,) + idx],
            recv_sem=sems.at[(1,) + idx],
            device_id=device,
            device_id_type=MESH,
        )

    def load_in(i):
        f = lax.rem(z + order[i], n_tp)
        r = pl.ds(pl.multiple_of(f * dc, dc), dc)
        s = i % n_w
        return (
            pltpu.make_async_copy(gate_hbm.at[r, :], gate_w.at[s], gate_sem.at[s]),
            pltpu.make_async_copy(up_hbm.at[r, :], up_w.at[s], up_sem.at[s]),
        )

    def load_down(i):
        f = lax.rem(z + out_order[i], n_tp)
        c = pl.ds(pl.multiple_of(f * dc, dc), dc)
        s = i % n_w
        return pltpu.make_async_copy(down_hbm.at[:, c], down_w.at[s], down_sem.at[s])

    for i in range(n_w):
        for c in load_in(i):
            c.start()

    barrier = pltpu.get_barrier_semaphore()
    pl.semaphore_signal(barrier, inc=1, device_id={"exp": partner}, device_id_type=MESH)
    for p in peers:
        pl.semaphore_signal(
            barrier, inc=1, device_id={"exp": p * CORES + core}, device_id_type=MESH
        )
    for d in range(1, n_tp):
        pl.semaphore_signal(
            barrier, inc=1, device_id={"tp": lax.rem(z + d, n_tp)}, device_id_type=MESH
        )

    rows[0, mine, :] = tok_ref[...]
    lane = lax.broadcasted_iota(jnp.int32, (tok, 128), 1)
    diff = log_ref[:, 0:1] - log_ref[:, 1:2]
    share[0, x] = jnp.where(ids_ref[:, 0:1] == lane, jax.nn.sigmoid(diff), 0.0) + jnp.where(
        ids_ref[:, 1:2] == lane, jax.nn.sigmoid(-diff), 0.0
    )
    pl.semaphore_wait(barrier, 1 + (n_x - 1) + (n_tp - 1))

    sends = []

    def send(copy):
        copy.start()
        sends.append(copy)
        return copy

    z_in = [None] + [
        send(
            remote(
                tok_ref,
                rows.at[i, mine, :],
                in_z,
                (i,),
                {"tp": lax.rem(z + n_tp - order[i], n_tp)},
            )
        )
        for i in range(1, n_tp)
    ]
    x_in = {}

    def send_x(i):
        if i >= n_tp:
            return
        if i > 0:
            z_in[i].wait_recv()
        src = tok_ref if i == 0 else rows.at[i, mine, :]
        x_in[i] = [
            send(
                remote(
                    src, rows.at[i, mine, :], in_x, (i, k), {"exp": p * CORES + core}
                )
            )
            for k, p in enumerate(peers)
        ]

    send_x(0)
    send_x(1)
    tn = tile_of(width)
    share_in = None
    for i in range(n_tp):
        for c in x_in[i]:
            c.wait_recv()
        relay = send(
            remote(
                rows.at[i, pl.ds(0, half), :],
                rows.at[i, pl.ds(half, half), :],
                in_p,
                (i,),
                {"exp": partner},
            )
        )
        send_x(i + 2)
        if i == n_tp - 1:
            share_in = [
                send(
                    remote(
                        share.at[0, x], share.at[0, x], share_x, (k,), {"exp": p * CORES + core}
                    )
                )
                for k, p in enumerate(peers)
            ]
        relay.wait_recv()
        for c in load_in(i):
            c.wait()
        s = i % n_w

        @pl.loop(0, width // tn)
        def _(t, i=i, s=s):
            cols = pl.ds(pl.multiple_of(t * tn, tn), tn)
            a = rows[i]
            g = jnp.dot(a, gate_w[s, :, cols], preferred_element_type=F32)
            u = jnp.dot(a, up_w[s, :, cols], preferred_element_type=F32)
            if i > 0:
                g = g + acc_g[:, cols]
                u = u + acc_u[:, cols]
            if i < n_tp - 1:
                acc_g[:, cols] = g
                acc_u[:, cols] = u
            else:
                hidden[:, cols] = (g * jax.nn.sigmoid(g) * u).astype(BF16)

        if i + n_w < n_tp:
            for c in load_in(i + n_w):
                c.start()
        if i == max(n_tp - n_w - 1, 0):
            for j in range(n_w):
                load_down(j).start()

    for c in share_in:
        c.wait_recv()
    share_relay = send(
        remote(share.at[0], share.at[1], share_p, (0,), {"exp": partner})
    )
    share_relay.wait_recv()
    groups = n_exp // EXPERTS
    expert = me // groups
    lanes = lax.broadcasted_iota(jnp.int32, (CORES * half, 128), 1)
    wall = share[...].reshape(CORES * half, 128)
    wcol[...] = jnp.broadcast_to(
        jnp.sum(jnp.where(lanes == expert, wall, 0.0), axis=1, keepdims=True), wcol.shape
    )

    to = tile_of(dc)
    to_partner = {}
    to_x = {}
    to_z = {}

    def compute(i):
        load_down(i).wait()
        s = i % n_w

        @pl.loop(0, dc // to)
        def _(t):
            cols = pl.ds(pl.multiple_of(t * to, to), to)
            p = jnp.dot(hidden[...], down_w[s, :, cols], preferred_element_type=F32)
            p = p * wcol[:, 0:1]
            comb[i, :, cols] = p[:half].astype(BF16)
            psend[i, :, cols] = p[half:].astype(BF16)

        if i + n_w < n_tp:
            load_down(i + n_w).start()
        to_partner[i] = send(
            remote(psend.at[i], precv.at[i], out_p, (i,), {"exp": partner})
        )

    def combine(i):
        to_partner[i].wait_recv()
        comb[i] = (comb[i].astype(F32) + precv[i].astype(F32)).astype(BF16)
        to_x[i] = [
            send(
                remote(
                    comb.at[i, pl.ds(pl.multiple_of(p * tok, tok), tok), :],
                    xrecv.at[i, k],
                    out_x,
                    (i, k),
                    {"exp": p * CORES + core},
                )
            )
            for k, p in enumerate(peers)
        ]

    def home(i):
        total = comb[i, mine, :].astype(F32)
        for k, c in enumerate(to_x[i]):
            c.wait_recv()
            total = total + xrecv[i, k].astype(F32)
        d = out_order[i]
        if d == 0:
            return total
        zsend[i] = total.astype(BF16)
        to_z[i] = send(
            remote(zsend.at[i], zrecv.at[i], out_z, (i,), {"tp": lax.rem(z + d, n_tp)})
        )

    own = None
    lag = 3
    for i in range(n_tp + lag):
        if i < n_tp:
            compute(i)
        if 0 <= i - 1 < n_tp:
            combine(i - 1)
        if 0 <= i - lag < n_tp:
            r = home(i - lag)
            own = r if r is not None else own
    for i in to_z:
        to_z[i].wait_recv()
        own = own + zrecv[i].astype(F32)
    out_ref[...] = own.astype(BF16)
    for c in sends:
        c.wait_send()


def on_device(tokens, expert_ids, route_logits, gate_weight, up_weight, down_weight):
    n_exp = lax.axis_size("exp")
    n_tp = lax.axis_size("tp")
    n_x = n_exp // CORES
    tok, dc = tokens.shape
    width = gate_weight.shape[1]
    n_w = min(n_tp, 3)
    total = n_exp * tok
    half = n_x * tok
    dma = pltpu.SemaphoreType.DMA
    vmem = pl.BlockSpec(memory_space=pltpu.VMEM)
    hbm = pl.BlockSpec(memory_space=pl.ANY)
    return pl.pallas_call(
        functools.partial(kernel, n_exp, n_tp, n_w),
        out_shape=jax.ShapeDtypeStruct((tok, dc), BF16),
        in_specs=[vmem, vmem, vmem, hbm, hbm, hbm],
        out_specs=vmem,
        scratch_shapes=[
            pltpu.VMEM((n_w, dc, width), BF16),
            pltpu.VMEM((n_w, dc, width), BF16),
            pltpu.VMEM((n_w, width, dc), BF16),
            pltpu.VMEM((n_tp, total, dc), BF16),
            pltpu.VMEM((total, width), F32),
            pltpu.VMEM((total, width), F32),
            pltpu.VMEM((total, width), BF16),
            pltpu.VMEM((CORES, n_x, tok, 128), F32),
            pltpu.VMEM((total, 128), F32),
            pltpu.VMEM((n_tp, half, dc), BF16),
            pltpu.VMEM((n_tp, half, dc), BF16),
            pltpu.VMEM((n_tp, half, dc), BF16),
            pltpu.VMEM((n_tp, n_x - 1, tok, dc), BF16),
            pltpu.VMEM((n_tp, tok, dc), BF16),
            pltpu.VMEM((n_tp, tok, dc), BF16),
            dma((n_w,)),
            dma((n_w,)),
            dma((n_w,)),
            dma((2, n_tp)),
            dma((2, n_tp, n_x - 1)),
            dma((2, n_tp)),
            dma((2, n_x - 1)),
            dma((2, 1)),
            dma((2, n_tp)),
            dma((2, n_tp, n_x - 1)),
            dma((2, n_tp)),
        ],
        compiler_params=pltpu.CompilerParams(
            collective_id=0, has_side_effects=True, vmem_limit_bytes=67043328
        ),
    )(tokens, expert_ids, route_logits, gate_weight, up_weight, down_weight)


def solution(mesh):
    return jax.shard_map(
        on_device,
        mesh=mesh,
        in_specs=(
            P(("rep", "exp"), "tp"),
            P(("rep", "exp"), None),
            P(("rep", "exp"), None),
            P(None, ("exp", "tp")),
            P(None, ("exp", "tp")),
            P(("exp", "tp"), None),
        ),
        out_specs=P(("rep", "exp"), "tp"),
        check_vma=False,
    )
```

time: 125 us -> 52.7 us (0.42)
  Pallas kernels: 0 us -> 48.3 us
  waiting for transfers between devices: 36.2 us -> 0 us
  blocking collectives: 34.9 us -> 0 us
  matrix products: 32.5 us -> 0 us
  between operations: 13.5 us -> 0.01 us
  starting transfers between devices: 3.45 us -> 0 us
  local copies, waits for them, and re-layouts: 1.89 us -> 4.26 us
  other arithmetic: 2.17 us -> 0 us
    pallas_call x0 -> x1, Pallas kernels: none -> 48.3 us  [on_device(): pl.pallas_call(functools.partial(kernel, n_exp, n_tp, n_w), out_shape=jax...]
    dot_general x6 -> x0, matrix products: 32.5 us -> none  [the longest x1 19.9 us: on_device(): jnp.dot(hidden, down_weight, preferred_element_type=jnp.float32)]
    reduce_scatter x1 -> x0, waiting for transfers between devices: 30.1 us -> none  [on_device(): lax.psum_scatter(partial_value.astype(jnp.float32).astype(jnp.bfloat16),...]
    all_to_all x1 -> x0, blocking collectives: 18.4 us -> none  [on_device(): lax.all_to_all(outgoing, 'exp', split_axis=0, concat_axis=0, tiled=True)]
    all_gather x1 -> x0, blocking collectives: 16.5 us -> none  [on_device(): whole_rows = lax.all_gather(tokens, 'tp', axis=1, tiled=True)]
    all_to_all x1 -> x0, waiting for transfers between devices: 6.06 us -> none  [on_device(): lax.all_to_all(narrow.astype(jnp.bfloat16), 'exp', split_axis=0, concat_a...]
    unnamed x4 -> x3, local copies, waits for them, and re-layouts: 0.01 us -> 4.26 us
    all_to_all x1 -> x0, starting transfers between devices: 3.45 us -> none  [on_device(): lax.all_to_all(narrow.astype(jnp.bfloat16), 'exp', split_axis=0, concat_a...]
  transfers between devices with their start and end apart: 2 -> 0, of which waited for: 2 -> 0; matrix products, arithmetic and copies ran while one was open for 0% -> 0% of each run, Pallas kernels for 0% -> 0%
where the time goes in v1:
time: 52.7 us; the launch traced here: 52.5 us
  Pallas kernels  48.3 us (92%)
  local copies, waits for them, and re-layouts  4.26 us (8%)
    pallas_call x1, Pallas kernels, on_device(): pl.pallas_call(functools.partial(kernel, n_exp, n_tp, n_w), out_shape=jax...  48.3 us
    unnamed x3, local copies, waits for them, and re-layouts  4.26 us

profile of v1, /device:TPU:0, one launch (start us, length us, event | category | flops | bytes accessed | tf_op | source)
XLA Modules:
  0.0 52.5 jit_solution(16110853752439738614)
XLA Ops:
  0.0 1.4 %copy.7.ids_ref = s32[32,2]{1,0:T(8,128)} copy(s32[32,2]{0,1:T(2,128)} %param.7) | data formatting | bytes 512 | tf_op args[1]
  1.4 1.4 %copy.8.log_ref = f32[32,2]{1,0:T(8,128)} copy(f32[32,2]{0,1:T(2,128)} %param.8) | data formatting | bytes 512 | tf_op args[2]
  2.7 48.3 %shard_map.64 = bf16[32,1536]{1,0:T(8,128)(2,1)} custom-call(bf16[32,1536]{1,0:T(8,128)(2,1)} %tok_ref.1, s32[32,2]{1,0:T(8,128)} %copy.7.ids_ref, f32[32,2]{1,0:T(8,128)} %copy.8.log_ref, bf16[6144,2048]{1,0:T(8,128)(2,1)} %gate_hbm.1, bf16[6144,2048]{1,0:T(8,128)(2,1)} %up_hbm.1, bf16[2048,6144]{1,0:T(8,128)(2,1)} %down_hbm.1), custom_call_target="tpu_custom_call" | custom-call | tf_op jit(solution)/shard_map/pallas_call | solution.py:315
  51.0 1.5 %copy.10 = bf16[32,1536]{1,0:T(8,128)(2,1)} copy(bf16[32,1536]{1,0:T(8,128)(2,1)} %shard_map.64) | data formatting | bytes 196608

commit v2 on v1

--- a/solution.py
+++ b/solution.py
@@ -121,9 +121,19 @@
 
     rows[0, mine, :] = tok_ref[...]
     lane = lax.broadcasted_iota(jnp.int32, (tok, 128), 1)
-    diff = log_ref[:, 0:1] - log_ref[:, 1:2]
-    share[0, x] = jnp.where(ids_ref[:, 0:1] == lane, jax.nn.sigmoid(diff), 0.0) + jnp.where(
-        ids_ref[:, 1:2] == lane, jax.nn.sigmoid(-diff), 0.0
+    eye = lax.broadcasted_iota(jnp.int32, (tok, tok), 0) == lax.broadcasted_iota(
+        jnp.int32, (tok, tok), 1
+    )
+
+    def column(row):
+        spread = jnp.where(eye, jnp.broadcast_to(row, (tok, tok)), jnp.zeros_like(row))
+        return jnp.sum(spread, axis=1, keepdims=True)
+
+    diff = column(log_ref[0:1, :] - log_ref[1:2, :])
+    ids = ids_ref[...].astype(F32)
+    lane = lane.astype(F32)
+    share[0, x] = jnp.where(column(ids[0:1]) == lane, jax.nn.sigmoid(diff), 0.0) + jnp.where(
+        column(ids[1:2]) == lane, jax.nn.sigmoid(-diff), 0.0
     )
     pl.semaphore_wait(barrier, 1 + (n_x - 1) + (n_tp - 1))
 
@@ -167,10 +177,14 @@
     send_x(1)
     tn = tile_of(width)
     share_in = None
-    for i in range(n_tp):
+    relays = {}
+
+    def relay_rows(i):
+        if i >= n_tp:
+            return
         for c in x_in[i]:
             c.wait_recv()
-        relay = send(
+        relays[i] = send(
             remote(
                 rows.at[i, pl.ds(0, half), :],
                 rows.at[i, pl.ds(half, half), :],
@@ -180,6 +194,9 @@
             )
         )
         send_x(i + 2)
+
+    relay_rows(0)
+    for i in range(n_tp):
         if i == n_tp - 1:
             share_in = [
                 send(
@@ -189,13 +206,12 @@
                 )
                 for k, p in enumerate(peers)
             ]
-        relay.wait_recv()
+        relays[i].wait_recv()
         for c in load_in(i):
             c.wait()
         s = i % n_w
 
-        @pl.loop(0, width // tn)
-        def _(t, i=i, s=s):
+        def expert_in(t, i=i, s=s):
             cols = pl.ds(pl.multiple_of(t * tn, tn), tn)
             a = rows[i]
             g = jnp.dot(a, gate_w[s, :, cols], preferred_element_type=F32)
@@ -208,6 +224,12 @@
                 acc_u[:, cols] = u
             else:
                 hidden[:, cols] = (g * jax.nn.sigmoid(g) * u).astype(BF16)
+
+        middle = width // tn // 2
+        if middle:
+            pl.loop(0, middle)(expert_in)
+        relay_rows(i + 1)
+        pl.loop(middle, width // tn)(expert_in)
 
         if i + n_w < n_tp:
             for c in load_in(i + n_w):
@@ -348,7 +370,7 @@
         compiler_params=pltpu.CompilerParams(
             collective_id=0, has_side_effects=True, vmem_limit_bytes=67043328
         ),
-    )(tokens, expert_ids, route_logits, gate_weight, up_weight, down_weight)
+    )(tokens, expert_ids.T, route_logits.T, gate_weight, up_weight, down_weight)
 
 
 def solution(mesh):

time: 52.7 us -> 50.7 us (0.962)
  local copies, waits for them, and re-layouts: 4.26 us -> 1.54 us
  Pallas kernels: 48.3 us -> 48.9 us
    unnamed x3 -> x1, local copies, waits for them, and re-layouts: 4.26 us -> 1.54 us
    pallas_call x1, Pallas kernels: 48.3 us -> 48.9 us  [on_device(): pl.pallas_call(functools.partial(kernel, n_exp, n_tp, n_w), out_shape=jax...]
where the time goes in v2:
time: 50.7 us; the launch traced here: 50.5 us
  Pallas kernels  48.9 us (96%)
  local copies, waits for them, and re-layouts  1.54 us (3%)
    pallas_call x1, Pallas kernels, on_device(): pl.pallas_call(functools.partial(kernel, n_exp, n_tp, n_w), out_shape=jax...  48.9 us
    unnamed x1, local copies, waits for them, and re-layouts  1.54 us

profile of v2, /device:TPU:0, one launch (start us, length us, event | category | flops | bytes accessed | tf_op | source)
XLA Modules:
  0.0 50.5 jit_solution(13249063887417911783)
XLA Ops:
  0.0 48.9 %shard_map.64 = bf16[32,1536]{1,0:T(8,128)(2,1)} custom-call(bf16[32,1536]{1,0:T(8,128)(2,1)} %tok_ref.1, s32[2,32]{1,0:T(2,128)} %bitcast.2, f32[2,32]{1,0:T(2,128)} %bitcast.3, bf16[6144,2048]{1,0:T(8,128)(2,1)} %gate_hbm.1, bf16[6144,2048]{1,0:T(8,128)(2,1)} %up_hbm.1, bf16[2048,6144]{1,0:T(8,128)(2,1)} %down_hbm.1), custom_call_target="tpu_custom_call" | custom-call | tf_op jit(solution)/shard_map/pallas_call | solution.py:337
  49.0 1.5 %copy.8 = bf16[32,1536]{1,0:T(8,128)(2,1)} copy(bf16[32,1536]{1,0:T(8,128)(2,1)} %shard_map.64) | data formatting | bytes 196608
